TPU v7x, 16 devices: a 4x2x1 block of a 4x4x8 slice. The times are simulated.
16 devices in a mesh: dp: 4 (over y, z, core), tp: 4 (over x).
Axes of the slice: x: 4, y: 2, z: 1, core: 2. Of those that a mesh axis runs over, the one named last changes fastest.
The devices are a block of a 4x4x8 slice.
Arguments:
- x: bfloat16 [512, 3072], P('dp'), parts along dimension 0
- w_gate: bfloat16 [3072, 8192], P(None, 'tp')
- w_up: bfloat16 [3072, 8192], P(None, 'tp')
- w_down: bfloat16 [8192, 3072], P('tp')
Outputs:
- output: bfloat16 [512, 3072], P('dp'), parts along dimension 0
There are 4 independent parts. A program takes and returns all parts, laid end to end along the dimension named above; an argument that names none is the same for every part.
All inputs are finite; a program needn't handle non-finite values.
Results may differ from a plain program's by a relative error of at most 0.016.
Values are sent between devices in bfloat16 or wider.
A program may use at most 768 MiB of HBM per device.

v0:
```python
import jax
import jax.numpy as jnp
from jax import lax
from jax.sharding import PartitionSpec as P


def solution(mesh):
    def step(x, w_gate, w_up, w_down):
        gate = jnp.dot(x, w_gate, preferred_element_type=jnp.float32)
        up = jnp.dot(x, w_up, preferred_element_type=jnp.float32)
        hidden = (jax.nn.silu(gate) * up).astype(jnp.bfloat16)
        term = jnp.dot(hidden, w_down, preferred_element_type=jnp.float32).astype(jnp.bfloat16)
        return lax.psum(term, "tp")

    return jax.shard_map(
        step,
        mesh=mesh,
        in_specs=(P("dp", None), P(None, "tp"), P(None, "tp"), P("tp", None)),
        out_specs=P("dp", None),
        check_vma=False,
    )
```

profile of v0, /device:TPU:112, one launch (start us, length us, event | category | flops | bytes accessed | tf_op | source)
XLA Modules:
  0.0 75.2 jit_solution(7642725930347507693)
XLA Ops:
  6.5 0.0 copy-start
  6.6 0.0 all-reduce.2.cloned.1.call-start
  6.6 1.1 %copy-done = bf16[128,3072]{1,0:T(8,128)(2,1)S(1)} copy-done((bf16[128,3072]{1,0:T(8,128)(2,1)S(1)}, bf16[128,3072]{1,0:T(8,128)(2,1)}, u32[]{:S(2)}) %copy-start) | copy-done | bytes 786456
  7.7 6.4 %fusion.3 = f32[128,2048]{1,0:T(8,128)S(1)} fusion(bf16[128,3072]{1,0:T(8,128)(2,1)S(1)} %copy-done, bf16[3072,2048]{1,0:T(8,128)(2,1)} %param.5), kind=kOutput, calls=%fused_computation.5 | convolution fusion | flops 1610612736 | bytes 14417920 | tf_op jit(solution)/shard_map/dot_general | solution.py:9
  14.1 12.6 %convolution_convert_fusion = bf16[128,3072]{1,0:T(8,128)(2,1)} fusion(bf16[2048,3072]{1,0:T(8,128)(2,1)} %param.7, bf16[128,3072]{1,0:T(8,128)(2,1)S(1)} %copy-done, bf16[3072,2048]{1,0:T(8,128)(2,1)} %param.6, f32[128,2048]{1,0:T(8,128)S(1)} %fusion.3), kind=kOutput, calls=%fused_computation | convolution fusion | flops 3223191552 | bytes 27787264 | tf_op jit(solution)/shard_map/dot_general | solution.py:12
  26.7 0.1 all-reduce.2.cloned.1.call-update
  26.8 39.5 %all-reduce.2.cloned.1.call-done = bf16[128,3072]{1,0:T(8,128)(2,1)} async-done(((bf16[128,3072]{1,0:T(8,128)(2,1)}), bf16[128,3072]{1,0:T(8,128)(2,1)}) %all-reduce.2.cloned.1.call-update) | async-done | bytes 786448 | tf_op jit(solution)/shard_map/psum | solution.py:13
  66.3 2.1 %copy.6 = bf16[128,3072]{1,0:T(8,128)(2,1)} copy(bf16[128,3072]{1,0:T(8,128)(2,1)} %all-reduce.2.cloned.1.call-done) | data formatting | bytes 1572864
Async XLA Ops:
  6.5 1.1 %copy-start = (bf16[128,3072]{1,0:T(8,128)(2,1)S(1)}, bf16[128,3072]{1,0:T(8,128)(2,1)}, u32[]{:S(2)}) copy-start(bf16[128,3072]{1,0:T(8,128)(2,1)} %param.4) | copy-start | bytes 2359300
  6.6 59.7 %all-reduce.2.cloned.1.call-start = ((), (), s32[]{:S(2)}) async-start(), calls=%async_computation | async-start | bytes 1572864 | tf_op jit(solution)/shard_map/psum | solution.py:13
Sparse Core Ops, SparseCore 0:
  26.9 39.3 all-reduce.1
where the time goes:
time: 75.4 us; the launch traced here: 75.2 us
  waiting for transfers between devices  39.6 us (53%)
  matrix products  19 us (25%)
  between operations  13.4 us (18%)
  local copies, waits for them, and re-layouts  3.19 us (4%)
    psum x1, waiting for transfers between devices, step(): return lax.psum(term, 'tp')  39.5 us
    dot_general x1, matrix products, step(): jnp.dot(hidden, w_down, preferred_element_type=jnp.float32)  12.6 us
    dot_general x1, matrix products, step(): gate = jnp.dot(x, w_gate, preferred_element_type=jnp.float32)  6.37 us
    unnamed x3, local copies, waits for them, and re-layouts  3.19 us
  transfers between devices with their start and end apart: 1, of which 1 were waited for; matrix products, arithmetic and copies ran while one was open for 0% of the time, Pallas kernels for 0%

commit v1 on v0

v1 whole, which is shorter than its diff:
```python
import functools

import jax
import jax.numpy as jnp
from jax import lax
from jax.experimental import pallas as pl
from jax.experimental.pallas import tpu as pltpu
from jax.sharding import PartitionSpec as P

MESH = pl.DeviceIdType.MESH
BN = 256
BC = 256
RIGHT, LEFT = 0, 1


def kernel(
    tp,
    x_hbm, wg_hbm, wu_hbm, wd_hbm,
    out,
    xs, wg, wu, wd, hid, hsend, fsend, frecv, rsend, lsend, from_left, from_right, sterm, oterm,
    xsem, gsem, usem, dsem, xrem, hrem, fs, fr, ss, sr, os_, or_, gas, gar, gbs, gbr, hs, hr,
):
    rows, depth = x_hbm.shape
    top = rows // 2
    nj = wg.shape[0]
    fh = nj * BN
    chunk = depth // tp
    nb = chunk // BC

    me = lax.axis_index("tp")
    dp = lax.axis_index("dp")
    core = lax.rem(dp, 2)
    partner = dp + 1 - 2 * core
    right, left = lax.rem(me + 1, tp), lax.rem(me + tp - 1, tp)
    to_right, to_left, to_partner = {"tp": right}, {"tp": left}, {"dp": partner}

    x_copy = pltpu.make_async_copy(x_hbm, xs.at[0], xsem)
    x_copy.start()
    gate_copies, up_copies = [], []
    for j in range(nj):
        cols = pl.ds(pl.multiple_of(core * fh + j * BN, BN), BN)
        gate_copies.append(pltpu.make_async_copy(wg_hbm.at[:, cols], wg.at[j], gsem.at[j]))
        up_copies.append(pltpu.make_async_copy(wu_hbm.at[:, cols], wu.at[j], usem.at[j]))
        gate_copies[j].start()
        up_copies[j].start()
    order = [(2, b) for b in range(nb)] + [(r, b) for b in range(nb) for r in (1, 3)] + [(0, b) for b in range(nb)]
    slot = {key: s for s, key in enumerate(order)}

    def columns(r, b):
        return pl.ds(pl.multiple_of(lax.rem(me + r, tp) * chunk + b * BC, BC), BC)

    down_copies = []
    for s, (r, b) in enumerate(order):
        pair = []
        for half in range(2):
            units = pl.ds(pl.multiple_of(lax.rem(core + half, 2) * fh, fh), fh)
            pair.append(
                pltpu.make_async_copy(
                    wd_hbm.at[units, columns(r, b)], wd.at[s, pl.ds(half * fh, fh)], dsem.at[s, half]
                )
            )
            pair[half].start()
        down_copies.append(pair)

    barrier = pltpu.get_barrier_semaphore()
    for device in (to_partner, to_right, to_left):
        pl.semaphore_signal(barrier, inc=1, device_id=device, device_id_type=MESH)
    x_copy.wait()
    pl.semaphore_wait(barrier, 3)

    def remote(src, dst, send, recv, device):
        return pltpu.make_async_remote_copy(
            src_ref=src, dst_ref=dst, send_sem=send, recv_sem=recv, device_id=device, device_id_type=MESH
        )

    x_remote = remote(xs.at[0], xs.at[1], xrem.at[0], xrem.at[1], to_partner)
    x_remote.start()

    waited = set()
    hidden_remote = []

    def block(j, other):
        if j not in waited:
            waited.add(j)
            gate_copies[j].wait()
            up_copies[j].wait()
        x = xs[1 if other else 0]
        gate = jnp.dot(x, wg[j], preferred_element_type=jnp.float32)
        up = jnp.dot(x, wu[j], preferred_element_type=jnp.float32)
        h = (jax.nn.silu(gate) * up).astype(jnp.bfloat16)
        if not other:
            hid[:, pl.ds(j * BN, BN)] = h
            return
        hsend[j] = h
        copy = remote(hsend.at[j], hid.at[:, pl.ds(fh + j * BN, BN)], hrem.at[0, j], hrem.at[1, j], to_partner)
        copy.start()
        hidden_remote.append(copy)

    block(0, False)
    block(1, False)
    x_remote.wait_recv()
    for j in range(nj):
        block(j, True)
    for j in range(2, nj):
        block(j, False)
    for copy in hidden_remote:
        copy.wait_recv()

    def term(r, b):
        s = slot[r, b]
        down_copies[s][0].wait()
        down_copies[s][1].wait()
        return jnp.dot(hid[...], wd[s], preferred_element_type=jnp.float32)

    A, B = pl.ds(0, top), pl.ds(top, top)
    sides = ((RIGHT, A, to_right), (LEFT, B, to_left))
    sends = []

    def go(copy):
        copy.start()
        sends.append(copy)
        return copy

    f = {}
    for b in range(nb):
        fsend[b] = term(2, b).astype(jnp.bfloat16)
        for d, part, device in sides:
            f[b, d] = go(remote(fsend.at[b, part], frecv.at[b, part], fs.at[b, d], fr.at[b, d], device))

    o, s_ = {}, {}

    def neighbour_terms(b):
        t = term(1, b)
        rsend[b, B] = t[top:].astype(jnp.bfloat16)
        sterm[b, A] = t[:top]
        t = term(3, b)
        lsend[b, A] = t[:top].astype(jnp.bfloat16)
        sterm[b, B] = t[top:]

    def send_o(b):
        o[b, RIGHT] = go(remote(rsend.at[b, B], from_left.at[b, B], os_.at[b, RIGHT], or_.at[b, RIGHT], to_right))
        o[b, LEFT] = go(remote(lsend.at[b, A], from_right.at[b, A], os_.at[b, LEFT], or_.at[b, LEFT], to_left))

    def send_s(b):
        f[b, RIGHT].wait_recv()
        rsend[b, A] = (sterm[b, A] + frecv[b, A].astype(jnp.float32)).astype(jnp.bfloat16)
        s_[b, RIGHT] = go(remote(rsend.at[b, A], from_left.at[b, A], ss.at[b, RIGHT], sr.at[b, RIGHT], to_right))
        f[b, LEFT].wait_recv()
        lsend[b, B] = (sterm[b, B] + frecv[b, B].astype(jnp.float32)).astype(jnp.bfloat16)
        s_[b, LEFT] = go(remote(lsend.at[b, B], from_right.at[b, B], ss.at[b, LEFT], sr.at[b, LEFT], to_left))

    for b in range(nb):
        neighbour_terms(b)
        if b < nb - 1:
            send_o(b)
    for b in range(nb):
        send_s(b)
        if b == 0:
            send_o(nb - 1)
        oterm[b] = term(0, b)

    ga, gb = {}, {}

    def finish(b):
        for d in (RIGHT, LEFT):
            s_[b, d].wait_recv()
            o[b, d].wait_recv()
        total = oterm[b] + from_left[b].astype(jnp.float32) + from_right[b].astype(jnp.float32)
        out[:, columns(0, b)] = total.astype(jnp.bfloat16)

    def send_ga(b):
        for d, part, device in sides:
            piece = out.at[part, columns(0, b)]
            ga[b, d] = go(remote(piece, piece, gas.at[b, d], gar.at[b, d], device))

    def send_gb(b):
        for d, part, device in ((RIGHT, B, to_right), (LEFT, A, to_left)):
            piece = out.at[part, columns(0, b)]
            gb[b, d] = go(remote(piece, piece, gbs.at[b, d], gbr.at[b, d], device))

    h_ = {}

    def pass_on(b):
        for d, part, device, owner in ((RIGHT, A, to_right, tp - 1), (LEFT, B, to_left, 1)):
            ga[b, d].wait_recv()
            piece = out.at[part, columns(owner, b)]
            h_[b, d] = go(remote(piece, piece, hs.at[b, d], hr.at[b, d], device))

    for b in range(nb):
        finish(b)
        send_ga(b)
        if b < nb - 1:
            send_gb(b)
    for b in range(nb):
        pass_on(b)
        if b == 0:
            send_gb(nb - 1)
    for b in range(nb):
        for d in (RIGHT, LEFT):
            gb[b, d].wait_recv()
            h_[b, d].wait_recv()
    x_remote.wait_send()
    for copy in hidden_remote:
        copy.wait_send()
    for copy in sends:
        copy.wait_send()


def solution(mesh):
    tp = mesh.shape["tp"]

    def step(x, w_gate, w_up, w_down):
        rows, depth = x.shape
        units = w_gate.shape[1]
        nj = units // 2 // BN
        nb = depth // tp // BC
        bf16, f32 = jnp.bfloat16, jnp.float32
        pieces = pltpu.VMEM((nb, rows, BC), bf16)
        dma = pltpu.SemaphoreType.DMA
        two = dma((nb, 2))
        return pl.pallas_call(
            functools.partial(kernel, tp),
            out_shape=jax.ShapeDtypeStruct((rows, depth), bf16),
            in_specs=[pl.BlockSpec(memory_space=pltpu.HBM)] * 4,
            out_specs=pl.BlockSpec(memory_space=pltpu.VMEM),
            scratch_shapes=[
                pltpu.VMEM((2, rows, depth), bf16),
                pltpu.VMEM((nj, depth, BN), bf16),
                pltpu.VMEM((nj, depth, BN), bf16),
                pltpu.VMEM((tp * nb, units, BC), bf16),
                pltpu.VMEM((rows, units), bf16),
                pltpu.VMEM((nj, rows, BN), bf16),
                pieces, pieces, pieces, pieces, pieces, pieces,
                pltpu.VMEM((nb, rows, BC), f32),
                pltpu.VMEM((nb, rows, BC), f32),
                dma, dma((nj,)), dma((nj,)), dma((tp * nb, 2)), dma((2,)), dma((2, nj)),
                two, two, two, two, two, two, two, two, two, two, two, two,
            ],
            compiler_params=pltpu.CompilerParams(collective_id=0, has_side_effects=True),
        )(x, w_gate, w_up, w_down)

    return jax.shard_map(
        step,
        mesh=mesh,
        in_specs=(P("dp", None), P(None, "tp"), P(None, "tp"), P("tp", None)),
        out_specs=P("dp", None),
        check_vma=False,
    )
```

time: 75.4 us -> 36.3 us (0.48)
  waiting for transfers between devices: 39.6 us -> 0 us
  Pallas kernels: 0 us -> 34.1 us
  matrix products: 19 us -> 0 us
  between operations: 13.4 us -> 0.01 us
  local copies, waits for them, and re-layouts: 3.19 us -> 2.06 us
    psum x1 -> x0, waiting for transfers between devices: 39.5 us -> none  [step(): return lax.psum(term, 'tp')]
    pallas_call x0 -> x1, Pallas kernels: none -> 34.1 us  [step(): pl.pallas_call(functools.partial(kernel, tp), out_shape=jax.ShapeDtypeStr...]
    dot_general x2 -> x0, matrix products: 19 us -> none  [the longest x1 12.6 us: step(): jnp.dot(hidden, w_down, preferred_element_type=jnp.float32)]
    unnamed x3 -> x1, local copies, waits for them, and re-layouts: 3.19 us -> 2.06 us
  transfers between devices with their start and end apart: 1 -> 0, of which waited for: 1 -> 0; matrix products, arithmetic and copies ran while one was open for 0% -> 0% of each run, Pallas kernels for 0% -> 0%
where the time goes in v1:
time: 36.3 us; the launch traced here: 36.2 us
  Pallas kernels  34.1 us (94%)
  local copies, waits for them, and re-layouts  2.06 us (6%)
    pallas_call x1, Pallas kernels, step(): pl.pallas_call(functools.partial(kernel, tp), out_shape=jax.ShapeDtypeStr...  34.1 us
    unnamed x1, local copies, waits for them, and re-layouts  2.06 us

profile of v1, /device:TPU:112, one launch (start us, length us, event | category | flops | bytes accessed | tf_op | source)
XLA Modules:
  0.0 36.2 jit_solution(6210998468447266984)
XLA Ops:
  0.0 34.1 %shard_map.46 = bf16[128,3072]{1,0:T(8,128)(2,1)} custom-call(bf16[128,3072]{1,0:T(8,128)(2,1)} %x_hbm.1, bf16[3072,2048]{1,0:T(8,128)(2,1)} %wg_hbm.1, bf16[3072,2048]{1,0:T(8,128)(2,1)} %wu_hbm.1, bf16[2048,3072]{1,0:T(8,128)(2,1)} %wd_hbm.1), custom_call_target="tpu_custom_call" | custom-call | tf_op jit(solution)/shard_map/pallas_call | solution.py:221
  34.1 2.1 %copy.6 = bf16[128,3072]{1,0:T(8,128)(2,1)} copy(bf16[128,3072]{1,0:T(8,128)(2,1)} %shard_map.46) | data formatting | bytes 1572864

commit v2 on v1

v2 whole, which is shorter than its diff:
```python
import functools

import jax
import jax.numpy as jnp
from jax import lax
from jax.experimental import pallas as pl
from jax.experimental.pallas import tpu as pltpu
from jax.sharding import PartitionSpec as P

MESH = pl.DeviceIdType.MESH
BN = 256
BC = 256
RIGHT, LEFT = 0, 1


def kernel(
    tp,
    x_hbm, wg_hbm, wu_hbm, wd_hbm,
    out,
    xs, wg, wu, wd, hid, hsend, fsend, frecv, rsend, lsend, from_left, from_right, sterm, oterm,
    xsem, gsem, usem, dsem, xrem, hrem, fs, fr, ss, sr, os_, or_, gas, gar, gbs, gbr, hs, hr,
):
    rows, depth = x_hbm.shape
    top = rows // 2
    nj = wg.shape[0]
    fh = nj * BN
    chunk = depth // tp
    nb = chunk // BC

    me = lax.axis_index("tp")
    dp = lax.axis_index("dp")
    core = lax.rem(dp, 2)
    partner = dp + 1 - 2 * core
    right, left = lax.rem(me + 1, tp), lax.rem(me + tp - 1, tp)
    to_right, to_left, to_partner = {"tp": right}, {"tp": left}, {"dp": partner}

    x_copy = pltpu.make_async_copy(x_hbm, xs.at[0], xsem)
    gate_copies, up_copies = [], []
    for j in range(nj):
        cols = pl.ds(pl.multiple_of(core * fh + j * BN, BN), BN)
        gate_copies.append(pltpu.make_async_copy(wg_hbm.at[:, cols], wg.at[j], gsem.at[j]))
        up_copies.append(pltpu.make_async_copy(wu_hbm.at[:, cols], wu.at[j], usem.at[j]))

    def columns(r, start, size):
        return pl.ds(pl.multiple_of(lax.rem(me + r, tp) * chunk + start, BC), size)

    down_copies = []
    for i, (r, start, size) in enumerate(((2, 0, BC), (2, BC, chunk - BC), (1, 0, chunk), (3, 0, chunk), (0, 0, chunk))):
        down_copies.append(
            pltpu.make_async_copy(
                wd_hbm.at[:, columns(r, start, size)], wd.at[r, :, pl.ds(start, size)], dsem.at[i]
            )
        )
    pending = [x_copy] + [c for j in range(nj) for c in (gate_copies[j], up_copies[j])] + down_copies

    def wait_read(copy):
        copy.wait()
        if pending:
            pending.pop(0).start()

    for _ in range(3):
        pending.pop(0).start()

    barrier = pltpu.get_barrier_semaphore()
    for device in (to_partner, to_right, to_left):
        pl.semaphore_signal(barrier, inc=1, device_id=device, device_id_type=MESH)
    with jax.named_scope('x_wait'):
        wait_read(x_copy)
    with jax.named_scope('barrier'):
        pl.semaphore_wait(barrier, 3)

    def remote(src, dst, send, recv, device):
        return pltpu.make_async_remote_copy(
            src_ref=src, dst_ref=dst, send_sem=send, recv_sem=recv, device_id=device, device_id_type=MESH
        )

    x_remote = remote(xs.at[0], xs.at[1], xrem.at[0], xrem.at[1], to_partner)
    x_remote.start()

    waited = set()
    hidden_remote = []

    def block(j, other):
        if j not in waited:
            waited.add(j)
            wait_read(gate_copies[j])
            wait_read(up_copies[j])
        x = xs[1 if other else 0]
        units = pl.ds(pl.multiple_of(core * fh + j * BN, BN), BN)
        gate = jnp.dot(x, wg[j], preferred_element_type=jnp.float32)
        up = jnp.dot(x, wu[j], preferred_element_type=jnp.float32)
        h = (jax.nn.silu(gate) * up).astype(jnp.bfloat16)
        if not other:
            hid[:, units] = h
            return
        hsend[j] = h
        copy = remote(hsend.at[j], hid.at[:, units], hrem.at[0, j], hrem.at[1, j], to_partner)
        copy.start()
        hidden_remote.append(copy)

    with jax.named_scope("own01"):
        block(0, False)
        block(1, False)
    with jax.named_scope("x_remote"):
        x_remote.wait_recv()
    with jax.named_scope("other"):
        for j in range(nj):
            block(j, True)
    with jax.named_scope("own23"):
        for j in range(2, nj):
            block(j, False)
    with jax.named_scope("hidden_remote"):
        for copy in hidden_remote:
            copy.wait_recv()

    def terms(*keys):
        out = []
        for r, b in keys:
            w = wd.at[r, :, pl.ds(b * BC, BC)]
            out.append(
                jnp.dot(hid[:, :fh], w[:fh], preferred_element_type=jnp.float32)
                + jnp.dot(hid[:, fh:], w[fh:], preferred_element_type=jnp.float32)
            )
        return out

    A, B = pl.ds(0, top), pl.ds(top, top)
    sides = ((RIGHT, A, to_right), (LEFT, B, to_left))
    sends = []

    def go(copy):
        copy.start()
        sends.append(copy)
        return copy

    f = {}

    def send_f(b):
        for d, part, device in sides:
            f[b, d] = go(remote(fsend.at[b, part], frecv.at[b, part], fs.at[b, d], fr.at[b, d], device))

    with jax.named_scope("f0"):
        wait_read(down_copies[0])
        fsend[0] = terms((2, 0))[0].astype(jnp.bfloat16)
        send_f(0)
    with jax.named_scope("f12"):
        wait_read(down_copies[1])
        for b, t in zip(range(1, nb), terms(*((2, b) for b in range(1, nb)))):
            fsend[b] = t.astype(jnp.bfloat16)
            send_f(b)

    o, s_ = {}, {}

    def neighbour_terms(b):
        t, u = terms((1, b), (3, b))
        rsend[b, B] = t[top:].astype(jnp.bfloat16)
        sterm[b, A] = t[:top]
        lsend[b, A] = u[:top].astype(jnp.bfloat16)
        sterm[b, B] = u[top:]

    def send_o(b):
        o[b, RIGHT] = go(remote(rsend.at[b, B], from_left.at[b, B], os_.at[b, RIGHT], or_.at[b, RIGHT], to_right))
        o[b, LEFT] = go(remote(lsend.at[b, A], from_right.at[b, A], os_.at[b, LEFT], or_.at[b, LEFT], to_left))

    def send_s(b):
        f[b, RIGHT].wait_recv()
        rsend[b, A] = (sterm[b, A] + frecv[b, A].astype(jnp.float32)).astype(jnp.bfloat16)
        s_[b, RIGHT] = go(remote(rsend.at[b, A], from_left.at[b, A], ss.at[b, RIGHT], sr.at[b, RIGHT], to_right))
        f[b, LEFT].wait_recv()
        lsend[b, B] = (sterm[b, B] + frecv[b, B].astype(jnp.float32)).astype(jnp.bfloat16)
        s_[b, LEFT] = go(remote(lsend.at[b, B], from_right.at[b, B], ss.at[b, LEFT], sr.at[b, LEFT], to_left))

    for b in range(nb):
        with jax.named_scope(f"neighbour{b}"):
            if b == 0:
                wait_read(down_copies[2])
                wait_read(down_copies[3])
            neighbour_terms(b)
            if b < nb - 1:
                send_o(b)
    with jax.named_scope("own_terms"):
        wait_read(down_copies[4])
        for b, t in enumerate(terms(*((0, b) for b in range(nb)))):
            oterm[b] = t
    for b in range(nb):
        with jax.named_scope(f"s{b}"):
            send_s(b)
            if b == 0:
                send_o(nb - 1)

    ga, gb = {}, {}

    def finish(b):
        for d in (RIGHT, LEFT):
            s_[b, d].wait_recv()
            o[b, d].wait_recv()
        total = oterm[b] + from_left[b].astype(jnp.float32) + from_right[b].astype(jnp.float32)
        out[:, columns(0, b * BC, BC)] = total.astype(jnp.bfloat16)

    def send_ga(b):
        for d, part, device in sides:
            piece = out.at[part, columns(0, b * BC, BC)]
            ga[b, d] = go(remote(piece, piece, gas.at[b, d], gar.at[b, d], device))

    def send_gb(b):
        for d, part, device in ((RIGHT, B, to_right), (LEFT, A, to_left)):
            piece = out.at[part, columns(0, b * BC, BC)]
            gb[b, d] = go(remote(piece, piece, gbs.at[b, d], gbr.at[b, d], device))

    h_ = {}

    def pass_on(b):
        for d, part, device, owner in ((RIGHT, A, to_right, tp - 1), (LEFT, B, to_left, 1)):
            ga[b, d].wait_recv()
            piece = out.at[part, columns(owner, b * BC, BC)]
            h_[b, d] = go(remote(piece, piece, hs.at[b, d], hr.at[b, d], device))

    finish_order = ["GA0", "GB0", "GA1", "GA2", "GB1", "H0", "GB2", "H1", "H2"]
    for step in finish_order:
        kind, b = step[:-1], int(step[-1])
        with jax.named_scope(step):
            if kind == "GA":
                finish(b)
                send_ga(b)
            elif kind == "GB":
                send_gb(b)
            else:
                pass_on(b)
    with jax.named_scope("last"):
        for b in range(nb):
            for d in (RIGHT, LEFT):
                gb[b, d].wait_recv()
                h_[b, d].wait_recv()
    with jax.named_scope("drain"):
        x_remote.wait_send()
        for copy in hidden_remote:
            copy.wait_send()
        for copy in sends:
            copy.wait_send()


def solution(mesh):
    tp = mesh.shape["tp"]

    def step(x, w_gate, w_up, w_down):
        rows, depth = x.shape
        units = w_gate.shape[1]
        nj = units // 2 // BN
        nb = depth // tp // BC
        bf16, f32 = jnp.bfloat16, jnp.float32
        pieces = pltpu.VMEM((nb, rows, BC), bf16)
        dma = pltpu.SemaphoreType.DMA
        two = dma((nb, 2))
        return pl.pallas_call(
            functools.partial(kernel, tp),
            out_shape=jax.ShapeDtypeStruct((rows, depth), bf16),
            in_specs=[pl.BlockSpec(memory_space=pltpu.HBM)] * 4,
            out_specs=pl.BlockSpec(memory_space=pltpu.VMEM),
            scratch_shapes=[
                pltpu.VMEM((2, rows, depth), bf16),
                pltpu.VMEM((nj, depth, BN), bf16),
                pltpu.VMEM((nj, depth, BN), bf16),
                pltpu.VMEM((tp, units, depth // tp), bf16),
                pltpu.VMEM((rows, units), bf16),
                pltpu.VMEM((nj, rows, BN), bf16),
                pieces, pieces, pieces, pieces, pieces, pieces,
                pltpu.VMEM((nb, rows, BC), f32),
                pltpu.VMEM((nb, rows, BC), f32),
                dma, dma((nj,)), dma((nj,)), dma((5,)), dma((2,)), dma((2, nj)),
                two, two, two, two, two, two, two, two, two, two, two, two,
            ],
            compiler_params=pltpu.CompilerParams(
                collective_id=0, has_side_effects=True, vmem_limit_bytes=40 * 2**20
            ),
        )(*(pltpu.with_memory_space_constraint(a, pltpu.HBM) for a in (x, w_gate, w_up, w_down)))

    return jax.shard_map(
        step,
        mesh=mesh,
        in_specs=(P("dp", None), P(None, "tp"), P(None, "tp"), P("tp", None)),
        out_specs=P("dp", None),
        check_vma=False,
    )
```

time: 36.3 us -> 28.9 us (0.80)
  Pallas kernels: 34.1 us -> 27.9 us
  local copies, waits for them, and re-layouts: 2.06 us -> 0.88 us
    pallas_call x1, Pallas kernels: 34.1 us -> 27.9 us  [step(): pl.pallas_call(functools.partial(kernel, tp), out_shape=jax.ShapeDtypeStr...]
    unnamed x1, local copies, waits for them, and re-layouts: 2.06 us -> 0.88 us
where the time goes in v2:
time: 28.9 us; the launch traced here: 28.8 us
  Pallas kernels  27.9 us (97%)
  local copies, waits for them, and re-layouts  0.88 us (3%)
    pallas_call x1, Pallas kernels, step(): pl.pallas_call(functools.partial(kernel, tp), out_shape=jax.ShapeDtypeStr...  27.9 us
    unnamed x1, local copies, waits for them, and re-layouts  0.88 us

profile of v2, /device:TPU:112, one launch (start us, length us, event | category | flops | bytes accessed | tf_op | source)
XLA Modules:
  0.0 28.8 jit_solution(18150622962673960734)
XLA Ops:
  0.0 27.9 %shard_map.46 = bf16[128,3072]{1,0:T(8,128)(2,1)S(1)} custom-call(bf16[128,3072]{1,0:T(8,128)(2,1)} %x_hbm.1, bf16[3072,2048]{1,0:T(8,128)(2,1)} %wg_hbm.1, bf16[3072,2048]{1,0:T(8,128)(2,1)} %wu_hbm.1, bf16[2048,3072]{1,0:T(8,128)(2,1)} %wd_hbm.1), custom_call_target="tpu_custom_call" | custom-call | tf_op jit(solution)/shard_map/pallas_call | solution.py:253
  27.9 0.9 %copy.6 = bf16[128,3072]{1,0:T(8,128)(2,1)} copy(bf16[128,3072]{1,0:T(8,128)(2,1)S(1)} %shard_map.46) | data formatting | bytes 1572864

commit v3 on v0

v3 whole, which is shorter than its diff:
```python
import functools

import jax
import jax.numpy as jnp
from jax import lax
from jax.experimental import pallas as pl
from jax.experimental.pallas import tpu as pltpu
from jax.sharding import PartitionSpec as P

MESH = pl.DeviceIdType.MESH
BN = 256
BC = 256
UNIT = 128
BATCHES = ((0, 1), (1, 1), (2, 1), (3, 1), (4, 2))
FIRST0 = ('g0', 'r4', 'm0', 'x0', 'p0', 'g1', 'r2', 'm1p1', 'g2', 'r1', 'h0', 'h1', 'p2', 'g3', 'h2', 'p3', 'h3', 'r1', 'm2m3')
FIRST1 = ('g0', 'r4', 'm0', 'g1', 'r2', 'm1', 'x0', 'p0p1', 'g2', 'r1', 'h0', 'h1', 'p2', 'g3', 'h2', 'p3', 'h3', 'r1', 'm2m3')
PLAN0 = ('c0', 'F2', 'c1', 'F4', 'F1', 'F3', 'F0', 'c2', 'O1', 'c3', 'O3', 'c4', 'O4', 'O2', 'S2', 'S4', 'O0', 'c5', 'S1', 'S3', 'S0', 'P2', 'Q2', 'P4', 'P1', 'P3', 'P0', 'Q1', 'Q0', 'Q3', 'H2', 'Q4', 'H4', 'H1', 'H3', 'H0')
PLAN1 = ('c0', 'F2', 'F0', 'F3', 'c1', 'c2', 'O0', 'c3', 'F4', 'S0', 'S2', 'F1', 'O2', 'c4', 'c5', 'O3', 'S3', 'P0', 'O4', 'S4', 'O1', 'Q0', 'P2', 'Q2', 'S1', 'P3', 'Q3', 'P4', 'H0', 'P1', 'Q1', 'Q4', 'H3', 'H2', 'H1', 'H4')


def kernel(
    tp,
    x_hbm, wg_hbm, wu_hbm, wd_hbm,
    out,
    xs, wgu, wd, hid, hsend, fsend, frecv, rsend, lsend, beside, sterm, oterm,
    reads, downs, far, arrived, sent,
):
    rows, depth = x_hbm.shape
    top = rows // 2
    nj = wgu.shape[0]
    fh = nj * BN
    chunk = depth // tp
    nb = chunk // BC
    nbatch = len(BATCHES)
    bf16, f32 = jnp.bfloat16, jnp.float32

    me = lax.axis_index("tp")
    dp = lax.axis_index("dp")
    core = lax.rem(dp, 2)
    partner = dp + 1 - 2 * core
    right, left = lax.rem(me + 1, tp), lax.rem(me + tp - 1, tp)
    to_right, to_left, to_partner = {"tp": right}, {"tp": left}, {"dp": partner}

    barrier = pltpu.get_barrier_semaphore()
    even = lax.rem(me, 2) == 0

    def greet(*devices):
        for device in devices:
            pl.semaphore_signal(barrier, inc=1, device_id=device, device_id_type=MESH)

    greet(to_partner)

    def remote(src, dst, send, recv, device):
        return pltpu.make_async_remote_copy(
            src_ref=src, dst_ref=dst, send_sem=send, recv_sem=recv, device_id=device, device_id_type=MESH
        )

    def wait(ref, sem):
        pltpu.make_async_copy(ref, ref, sem).wait()

    def units(j):
        return pl.ds(pl.multiple_of(core * fh + j * BN, BN), BN)

    def columns(r, start, size):
        return pl.ds(pl.multiple_of(lax.rem(me + r, tp) * chunk + start, UNIT), size)

    pending = [pltpu.make_async_copy(x_hbm, xs.at[0], reads.at[nj])]
    for j in range(nj):
        for i, w in enumerate((wg_hbm, wu_hbm)):
            pending.append(pltpu.make_async_copy(w.at[:, units(j)], wgu.at[j, i], reads.at[j]))
    downs_of = ((2, 0, 2 * BC), (2, 2 * BC, chunk - 2 * BC), (1, 0, chunk), (3, 0, chunk), (0, 0, chunk))
    for i, (r, start, size) in enumerate(downs_of):
        pending.append(
            pltpu.make_async_copy(wd_hbm.at[:, columns(r, start, size)], wd.at[r, :, pl.ds(start, size)], downs.at[i])
        )
    down_copies = pending[-len(downs_of) :]

    def start_reads(count):
        for _ in range(count):
            pending.pop(0).start()

    start_reads(3)
    with jax.named_scope("barrier"):
        pl.when(even)(lambda: pl.semaphore_wait(barrier, 1))
        pl.when(jnp.logical_not(even))(lambda: pl.semaphore_wait(barrier, 3))
        greet(to_right, to_left)
    with jax.named_scope("x_wait"):
        wait(xs.at[0], reads.at[nj])
        start_reads(2)
    x_remote = remote(xs.at[0], xs.at[1], far.at[0], far.at[1], to_partner)
    x_remote.start()

    def block(j, other):
        x = xs[1 if other else 0]
        gate = jnp.dot(x, wgu[j, 0], preferred_element_type=f32)
        up = jnp.dot(x, wgu[j, 1], preferred_element_type=f32)
        h = (jax.nn.silu(gate) * up).astype(bf16)
        if other:
            hsend[:, pl.ds(j * BN, BN)] = h
        else:
            hid[:, units(j)] = h

    def hidden(plan, later):
        for word in plan:
            with jax.named_scope(word):
                kind, j = word[0], int(word[1])
                if kind == "g":
                    wait(wgu.at[j], reads.at[j])
                elif kind == "x":
                    x_remote.wait_recv()
                elif kind == "h":
                    remote(
                        hsend.at[:, pl.ds(j * BN, BN)], hid.at[:, units(j)], far.at[2], far.at[3], to_partner
                    ).start()
                elif kind == "r":
                    for _ in range(j):
                        later.pop(0).start()
                else:
                    for i in range(0, len(word), 2):
                        block(int(word[i + 1]), word[i] == "p")
        with jax.named_scope("hidden_remote"):
            wait(hid.at[:, pl.ds(pl.multiple_of((1 - core) * fh, fh), fh)], far.at[3])
            pl.when(even)(lambda: pl.semaphore_wait(barrier, 2))

    A, B = pl.ds(0, top), pl.ds(top, top)
    sides = ((A, to_right), (B, to_left))
    others = ((B, to_right), (A, to_left))
    batches = [(UNIT * a, UNIT * n) for a, n in BATCHES]
    cols = [pl.ds(start, size) for start, size in batches]
    pieces = [(2, b) for b in range(nb)] + [(r, b) for b in range(nb) for r in (1, 3)] + [(0, b) for b in range(nb)]
    needs = {(2, 0): 0, (2, 2): 1, (1, 0): 2, (3, 0): 3, (0, 0): 4}

    def compute(i):
        pair = pieces[2 * i : 2 * i + 2]
        for key in pair:
            if key in needs:
                down_copies[needs[key]].wait()
                if needs[key] == 0:
                    down_copies[4].start()
        terms = [
            jnp.dot(hid[...], wd[r, :, pl.ds(b * BC, BC)], preferred_element_type=f32) for r, b in pair
        ]
        for (r, b), t in zip(pair, terms):
            at = pl.ds(b * BC, BC)
            if r == 2:
                fsend[:, at] = t.astype(bf16)
            elif r == 1:
                rsend[B, at] = t[top:].astype(bf16)
                sterm[A, at] = t[:top]
            elif r == 3:
                lsend[A, at] = t[:top].astype(bf16)
                sterm[B, at] = t[top:]
            else:
                oterm[:, at] = t

    def exchange(plan):
        def go(src, dst, which, device):
            remote(src, dst, sent, arrived.at[which], device).start()

        def out_piece(owner, b, part):
            return out.at[part, columns(owner, *batches[b])]

        def step(kind, b):
            if kind == "c":
                compute(b)
            elif kind == "F":
                for part, device in sides:
                    go(fsend.at[part, cols[b]], frecv.at[part, cols[b]], b, device)
            elif kind == "O":
                go(rsend.at[B, cols[b]], beside.at[0, B, cols[b]], nbatch + b, to_right)
                go(lsend.at[A, cols[b]], beside.at[1, A, cols[b]], nbatch + b, to_left)
            elif kind == "S":
                wait(frecv.at[:, cols[b]], arrived.at[b])
                total = (sterm[:, cols[b]] + frecv[:, cols[b]].astype(f32)).astype(bf16)
                rsend[A, cols[b]] = total[:top]
                lsend[B, cols[b]] = total[top:]
                go(rsend.at[A, cols[b]], beside.at[0, A, cols[b]], nbatch + b, to_right)
                go(lsend.at[B, cols[b]], beside.at[1, B, cols[b]], nbatch + b, to_left)
            elif kind == "P":
                wait(beside.at[:, :, cols[b]], arrived.at[nbatch + b])
                total = oterm[:, cols[b]] + beside[0, :, cols[b]].astype(f32) + beside[1, :, cols[b]].astype(f32)
                out[:, columns(0, *batches[b])] = total.astype(bf16)
                for part, device in sides:
                    go(out_piece(0, b, part), out_piece(0, b, part), 2 * nbatch + b, device)
            elif kind == "Q":
                for part, device in others:
                    go(out_piece(0, b, part), out_piece(0, b, part), 3 * nbatch, device)
            else:
                wait(frecv.at[:, cols[b]], arrived.at[2 * nbatch + b])
                for (part, device), owner in zip(sides, (tp - 1, 1)):
                    go(out_piece(owner, b, part), out_piece(owner, b, part), 3 * nbatch, device)

        for word in plan:
            with jax.named_scope(word):
                step(word[0], int(word[1:]))

    def run(first, plan):
        hidden(first, list(pending))
        exchange(plan)

    pl.when(core == 0)(lambda: run(FIRST0, PLAN0))
    pl.when(core == 1)(lambda: run(FIRST1, PLAN1))
    with jax.named_scope("last"):
        wait(beside, arrived.at[3 * nbatch])
    with jax.named_scope("drain"):
        x_remote.wait_send()
        wait(hsend, far.at[2])
        wait(wd.at[0, pl.ds(0, 6 * rows)], sent)


def solution(mesh):
    tp = mesh.shape["tp"]

    def step(x, w_gate, w_up, w_down):
        rows, depth = x.shape
        units = w_gate.shape[1]
        nj = units // 2 // BN
        chunk = depth // tp
        bf16, f32 = jnp.bfloat16, jnp.float32
        quarter = pltpu.VMEM((rows, chunk), bf16)
        dma = pltpu.SemaphoreType.DMA
        operands = [pltpu.with_memory_space_constraint(a, pltpu.HBM) for a in (x, w_gate, w_up, w_down)]
        return pl.pallas_call(
            functools.partial(kernel, tp),
            out_shape=jax.ShapeDtypeStruct((rows, depth), bf16),
            in_specs=[pl.BlockSpec(memory_space=pltpu.HBM)] * 4,
            out_specs=pl.BlockSpec(memory_space=pltpu.VMEM),
            scratch_shapes=[
                pltpu.VMEM((2, rows, depth), bf16),
                pltpu.VMEM((nj, 2, depth, BN), bf16),
                pltpu.VMEM((tp, units, chunk), bf16),
                pltpu.VMEM((rows, units), bf16),
                pltpu.VMEM((rows, units // 2), bf16),
                quarter, quarter, quarter, quarter,
                pltpu.VMEM((2, rows, chunk), bf16),
                pltpu.VMEM((rows, chunk), f32),
                pltpu.VMEM((rows, chunk), f32),
                dma((nj + 1,)), dma((5,)), dma((4,)), dma((3 * len(BATCHES) + 1,)), dma,
            ],
            compiler_params=pltpu.CompilerParams(
                collective_id=0, has_side_effects=True, vmem_limit_bytes=40 * 2**20
            ),
        )(*operands)

    return jax.shard_map(
        step,
        mesh=mesh,
        in_specs=(P("dp", None), P(None, "tp"), P(None, "tp"), P("tp", None)),
        out_specs=P("dp", None),
        check_vma=False,
    )
```

time: 75.4 us -> 26.7 us (0.35)
  the two profiles are of different devices: /device:TPU:112 before, /device:TPU:113 now
where the time goes in v3:
time: 26.7 us; the launch traced here: 26.6 us
  Pallas kernels  25.7 us (96%)
  local copies, waits for them, and re-layouts  0.88 us (3%)
    pallas_call x1, Pallas kernels, step(): pl.pallas_call(functools.partial(kernel, tp), out_shape=jax.ShapeDtypeStr...  25.7 us
    unnamed x1, local copies, waits for them, and re-layouts  0.88 us

profile of v3, /device:TPU:113, one launch (start us, length us, event | category | flops | bytes accessed | tf_op | source)
XLA Modules:
  0.0 26.6 jit_solution(3560487302450570169)
XLA Ops:
  0.0 25.7 %shard_map.46 = bf16[128,3072]{1,0:T(8,128)(2,1)S(1)} custom-call(bf16[128,3072]{1,0:T(8,128)(2,1)} %x_hbm.1, bf16[3072,2048]{1,0:T(8,128)(2,1)} %wg_hbm.1, bf16[3072,2048]{1,0:T(8,128)(2,1)} %wu_hbm.1, bf16[2048,3072]{1,0:T(8,128)(2,1)} %wd_hbm.1), custom_call_target="tpu_custom_call" | custom-call | tf_op jit(solution)/shard_map/pallas_call | solution.py:223
  25.8 0.9 %copy.6 = bf16[128,3072]{1,0:T(8,128)(2,1)} copy(bf16[128,3072]{1,0:T(8,128)(2,1)S(1)} %shard_map.46) | data formatting | bytes 1572864

commit v4 on v3

--- a/solution.py
+++ b/solution.py
@@ -14,8 +14,8 @@
 BATCHES = ((0, 1), (1, 1), (2, 1), (3, 1), (4, 2))
 FIRST0 = ('g0', 'r4', 'm0', 'x0', 'p0', 'g1', 'r2', 'm1p1', 'g2', 'r1', 'h0', 'h1', 'p2', 'g3', 'h2', 'p3', 'h3', 'r1', 'm2m3')
 FIRST1 = ('g0', 'r4', 'm0', 'g1', 'r2', 'm1', 'x0', 'p0p1', 'g2', 'r1', 'h0', 'h1', 'p2', 'g3', 'h2', 'p3', 'h3', 'r1', 'm2m3')
-PLAN0 = ('c0', 'F2', 'c1', 'F4', 'F1', 'F3', 'F0', 'c2', 'O1', 'c3', 'O3', 'c4', 'O4', 'O2', 'S2', 'S4', 'O0', 'c5', 'S1', 'S3', 'S0', 'P2', 'Q2', 'P4', 'P1', 'P3', 'P0', 'Q1', 'Q0', 'Q3', 'H2', 'Q4', 'H4', 'H1', 'H3', 'H0')
-PLAN1 = ('c0', 'F2', 'F0', 'F3', 'c1', 'c2', 'O0', 'c3', 'F4', 'S0', 'S2', 'F1', 'O2', 'c4', 'c5', 'O3', 'S3', 'P0', 'O4', 'S4', 'O1', 'Q0', 'P2', 'Q2', 'S1', 'P3', 'Q3', 'P4', 'H0', 'P1', 'Q1', 'Q4', 'H3', 'H2', 'H1', 'H4')
+PLAN0 = ('c0', 'F0', 'F1', 'c1', 'F2', 'F4', 'F3', 'c2', 'c3', 'c4', 'O2', 'O0', 'O4', 'c5', 'S0', 'S2', 'S4', 'S1', 'O1', 'S3', 'O3', 'P0', 'P2', 'Q2', 'P4', 'P1', 'Q0', 'P3', 'Q3', 'Q4', 'H2', 'Q1', 'H4', 'H0', 'H1', 'H3')
+PLAN1 = ('c0', 'F1', 'F0', 'c1', 'c2', 'F2', 'F4', 'c3', 'O2', 'F3', 'O1', 'S1', 'c4', 'O0', 'O3', 'S0', 'c5', 'S2', 'P1', 'S4', 'O4', 'S3', 'Q1', 'P0', 'P2', 'Q0', 'P4', 'P3', 'Q4', 'Q2', 'H0', 'H1', 'H2', 'Q3', 'H4', 'H3')
 
 
 def kernel(
@@ -127,19 +127,23 @@
     others = ((B, to_right), (A, to_left))
     batches = [(UNIT * a, UNIT * n) for a, n in BATCHES]
     cols = [pl.ds(start, size) for start, size in batches]
-    pieces = [(2, b) for b in range(nb)] + [(r, b) for b in range(nb) for r in (1, 3)] + [(0, b) for b in range(nb)]
+    steps = [[(2, 0)], [(2, b) for b in range(1, nb)]] + [[(1, b), (3, b)] for b in range(nb)] + [[(0, b) for b in range(nb)]]
     needs = {(2, 0): 0, (2, 2): 1, (1, 0): 2, (3, 0): 3, (0, 0): 4}
 
     def compute(i):
-        pair = pieces[2 * i : 2 * i + 2]
+        pair = steps[i]
         for key in pair:
             if key in needs:
                 down_copies[needs[key]].wait()
                 if needs[key] == 0:
                     down_copies[4].start()
-        terms = [
-            jnp.dot(hid[...], wd[r, :, pl.ds(b * BC, BC)], preferred_element_type=f32) for r, b in pair
-        ]
+        def product(r, b, half, sign):
+            return jnp.dot(sign * hid[:, half], wd[r, half, pl.ds(b * BC, BC)], preferred_element_type=f32)
+
+        if len(pair) == 1:
+            terms = [product(*pair[0], pl.ds(0, fh), 1) - product(*pair[0], pl.ds(fh, fh), -1)]
+        else:
+            terms = [product(r, b, slice(None), 1) for r, b in pair]
         for (r, b), t in zip(pair, terms):
             at = pl.ds(b * BC, BC)
             if r == 2:

time: 26.7 us -> 26.6 us (level)
  the two profiles are of different devices: /device:TPU:113 before, /device:TPU:112 now
where the time goes in v4:
time: 26.6 us; the launch traced here: 26.5 us
  Pallas kernels  25.6 us (96%)
  local copies, waits for them, and re-layouts  0.88 us (3%)
    pallas_call x1, Pallas kernels, step(): pl.pallas_call(functools.partial(kernel, tp), out_shape=jax.ShapeDtypeStr...  25.6 us
    unnamed x1, local copies, waits for them, and re-layouts  0.88 us

profile of v4, /device:TPU:112, one launch (start us, length us, event | category | flops | bytes accessed | tf_op | source)
XLA Modules:
  0.0 26.5 jit_solution(3991772939526091567)
XLA Ops:
  0.0 25.6 %shard_map.46 = bf16[128,3072]{1,0:T(8,128)(2,1)S(1)} custom-call(bf16[128,3072]{1,0:T(8,128)(2,1)} %x_hbm.1, bf16[3072,2048]{1,0:T(8,128)(2,1)} %wg_hbm.1, bf16[3072,2048]{1,0:T(8,128)(2,1)} %wu_hbm.1, bf16[2048,3072]{1,0:T(8,128)(2,1)} %wd_hbm.1), custom_call_target="tpu_custom_call" | custom-call | tf_op jit(solution)/shard_map/pallas_call | solution.py:227
  25.6 0.9 %copy.6 = bf16[128,3072]{1,0:T(8,128)(2,1)} copy(bf16[128,3072]{1,0:T(8,128)(2,1)S(1)} %shard_map.46) | data formatting | bytes 1572864

commit v5 on v4

--- a/solution.py
+++ b/solution.py
@@ -12,8 +12,8 @@
 BC = 256
 UNIT = 128
 BATCHES = ((0, 1), (1, 1), (2, 1), (3, 1), (4, 2))
-FIRST0 = ('g0', 'r4', 'm0', 'x0', 'p0', 'g1', 'r2', 'm1p1', 'g2', 'r1', 'h0', 'h1', 'p2', 'g3', 'h2', 'p3', 'h3', 'r1', 'm2m3')
-FIRST1 = ('g0', 'r4', 'm0', 'g1', 'r2', 'm1', 'x0', 'p0p1', 'g2', 'r1', 'h0', 'h1', 'p2', 'g3', 'h2', 'p3', 'h3', 'r1', 'm2m3')
+FIRST0 = ('g0', 'r4', 'm0', 'x0', 'p0', 'g1', 'r2', 'm1p1', 'g2', 'r1', 'p2', 'h0', 'h1', 'h2', 'g3', 'p3', 'h3', 'r1', 'm2m3')
+FIRST1 = ('g0', 'r4', 'm0', 'g1', 'x0', 'r2', 'm1p0', 'g2', 'r1', 'p1p2', 'h0', 'h1', 'h2', 'g3', 'p3', 'h3', 'r1', 'm2m3')
 PLAN0 = ('c0', 'F0', 'F1', 'c1', 'F2', 'F4', 'F3', 'c2', 'c3', 'c4', 'O2', 'O0', 'O4', 'c5', 'S0', 'S2', 'S4', 'S1', 'O1', 'S3', 'O3', 'P0', 'P2', 'Q2', 'P4', 'P1', 'Q0', 'P3', 'Q3', 'Q4', 'H2', 'Q1', 'H4', 'H0', 'H1', 'H3')
 PLAN1 = ('c0', 'F1', 'F0', 'c1', 'c2', 'F2', 'F4', 'c3', 'O2', 'F3', 'O1', 'S1', 'c4', 'O0', 'O3', 'S0', 'c5', 'S2', 'P1', 'S4', 'O4', 'S3', 'Q1', 'P0', 'P2', 'Q0', 'P4', 'P3', 'Q4', 'Q2', 'H0', 'H1', 'H2', 'Q3', 'H4', 'H3')
 

time: 26.6 us -> 26.5 us (level)
  no operation moved by 1% of the time
where the time goes in v5:
time: 26.5 us
  Pallas kernels  25.6 us (97%)
  local copies, waits for them, and re-layouts  0.88 us (3%)
    pallas_call x1, Pallas kernels, step(): pl.pallas_call(functools.partial(kernel, tp), out_shape=jax.ShapeDtypeStr...  25.6 us
    unnamed x1, local copies, waits for them, and re-layouts  0.88 us

profile of v5, /device:TPU:112, one launch (start us, length us, event | category | flops | bytes accessed | tf_op | source)
XLA Modules:
  0.0 26.5 jit_solution(11769246083788293557)
XLA Ops:
  0.0 25.6 %shard_map.46 = bf16[128,3072]{1,0:T(8,128)(2,1)S(1)} custom-call(bf16[128,3072]{1,0:T(8,128)(2,1)} %x_hbm.1, bf16[3072,2048]{1,0:T(8,128)(2,1)} %wg_hbm.1, bf16[3072,2048]{1,0:T(8,128)(2,1)} %wu_hbm.1, bf16[2048,3072]{1,0:T(8,128)(2,1)} %wd_hbm.1), custom_call_target="tpu_custom_call" | custom-call | tf_op jit(solution)/shard_map/pallas_call | solution.py:227
  25.6 0.9 %copy.6 = bf16[128,3072]{1,0:T(8,128)(2,1)} copy(bf16[128,3072]{1,0:T(8,128)(2,1)S(1)} %shard_map.46) | data formatting | bytes 1572864
